TPU v7x, 128 devices: a whole 4x4x4 slice. The times are simulated.
128 devices in a mesh: row: 8 (over z, core), col: 16 (over y, x).
Axes of the slice: x: 4, y: 4, z: 4, core: 2. Of those that a mesh axis runs over, the one named last changes fastest.
Arguments:
- grad_out: bfloat16 [131072, 256], P(('row', 'col')), may hold values from -6 to 6
- rel_weight: bfloat16 [4, 256, 256], replicated, may hold values from -0.375 to 0.375
- adjacency: bfloat16 [24576, 128, 128], P(('row', 'col')), may hold values from -0.5 to 0.5
- block_row: int32 [24576], P(('row', 'col')), may hold values from 0 to 127, as said below
- block_col: int32 [24576], P(('row', 'col')), may hold values from 0 to 63
- type_count: int32 [512], P(('row', 'col')), may hold values from 0 to 192, as said below
Outputs:
- grad_in: float32 [131072, 256], P(('row', 'col'))
Inputs may be any that keep to these rules, and one draw needn't show every extreme that they name: `block_row`: among all 192 slots of one tile, at most 4 distinct values fall in any aligned range of 8 values (the node blocks of one device of the tile row), and in every tile some range holds exactly 4. `type_count`: A tile's 4 counts sum to at most 192; in some tile a single type holds all 192 slots.
All inputs are finite; a program needn't handle non-finite values.
Results may differ from a plain program's by a relative error of at most 0.012.
Values may be sent and summed in bfloat16 or wider, within the bound.
A program may use at most 192 MiB of HBM per device.

v0:
```python
import math
import jax
import jax.numpy as jnp
from jax import lax
from jax.sharding import PartitionSpec as P


def per_device(grad_out, rel_weight, adjacency, block_row, block_col, type_count):
    ncols = lax.axis_size("col")
    nrows = lax.axis_size("row")
    blk = adjacency.shape[1]
    feat = grad_out.shape[1]
    kinds = rel_weight.shape[0]
    owned = grad_out.shape[0] // blk
    slots_total = adjacency.shape[0]
    wcat = jnp.transpose(rel_weight, (2, 0, 1)).reshape(feat, kinds * feat)
    gathered = jnp.dot(
        lax.all_gather(grad_out, "col", axis=0, tiled=True),
        wcat,
        preferred_element_type=jnp.float32,
    ).astype(jnp.bfloat16)
    table = gathered.reshape(ncols * owned, blk, kinds, feat)
    ends = jnp.cumsum(type_count)
    total = ends[kinds - 1]
    position = jnp.arange(slots_total, dtype=jnp.int32)
    kind = jnp.minimum(
        jnp.sum((position[:, None] >= ends[None, :]).astype(jnp.int32), axis=1), kinds - 1
    )
    live = position < total
    group = math.gcd(slots_total, 64)
    groups = slots_total // group
    partial_start = jnp.zeros((nrows * owned, blk, feat), jnp.float32)

    def step(index, partial_value):
        start = index * group
        adj_part = lax.dynamic_slice_in_dim(adjacency, start, group, 0)
        slot_part = lax.dynamic_slice_in_dim(block_row, start, group, 0)
        kind_part = lax.dynamic_slice_in_dim(kind, start, group, 0)
        live_part = lax.dynamic_slice_in_dim(live, start, group, 0)
        col_part = lax.dynamic_slice_in_dim(block_col, start, group, 0)
        picked = table[slot_part, :, kind_part, :]
        term = jnp.einsum("kab,kaf->kbf", adj_part, picked, preferred_element_type=jnp.float32)
        term = jnp.where(live_part[:, None, None], term, jnp.float32(0.0))
        return partial_value.at[col_part].add(term)

    partial_value = lax.fori_loop(0, groups, step, partial_start)
    return lax.psum_scatter(
        partial_value.reshape(nrows * owned * blk, feat).astype(jnp.bfloat16),
        "row",
        scatter_dimension=0,
        tiled=True,
    ).astype(jnp.float32)


def solution(mesh):
    in_specs = (
        P(("row", "col"), None),
        P(),
        P(("row", "col"), None, None),
        P(("row", "col")),
        P(("row", "col")),
        P(("row", "col")),
    )
    out_specs = P(("row", "col"), None)
    return jax.shard_map(
        per_device, mesh=mesh, in_specs=in_specs, out_specs=out_specs, check_vma=False
    )
```

profile of v0, /device:TPU:0, one launch (start us, length us, event | category | flops | bytes accessed | tf_op | source)
XLA Modules:
  0.0 332.7 jit_solution(6268306720380920505)
XLA Ops:
  6.5 0.0 copy-start
  6.5 0.0 all-gather.2.cloned.1.call-start
  6.5 0.7 all-gather.2.cloned.1.call-update
  7.3 0.0 reduce-scatter.2.cloned.1.call-start
  7.3 0.8 reduce-window.4
  8.1 0.6 slice.4
  8.7 0.6 iota_compare_fusion.1
  9.3 0.1 convert_reduce_fusion
  9.4 73.3 %all-gather.2.cloned.1.call-done = bf16[16384,256]{1,0:T(8,128)(2,1)} async-done(((bf16[1024,256]{1,0:T(8,128)(2,1)}), bf16[16384,256]{1,0:T(8,128)(2,1)}) %all-gather.2.cloned.1.call-update) | async-done | bytes 8388624 | tf_op jit(solution)/shard_map/all_gather | solution.py:18
  82.7 0.0 copy-done
  82.7 17.5 %convolution_convert_fusion = bf16[16384,1024]{1,0:T(8,128)(2,1)} fusion(bf16[16384,256]{1,0:T(8,128)(2,1)} %all-gather.2.cloned.1.call-done, bf16[256,1024]{0,1:T(8,128)(2,1)S(1)} %bitcast.12), kind=kOutput, calls=%fused_computation.13 | convolution fusion | flops 8606711808 | bytes 42467328 | tf_op jit(solution)/shard_map/dot_general | solution.py:17
  100.1 54.7 %reshape.19 = bf16[128,128,4,256]{3,2,1,0:T(4,128)(2,1)} reshape(bf16[16384,1024]{1,0:T(8,128)(2,1)} %convolution_convert_fusion) | data formatting | bytes 67108864 | tf_op jit(solution)/shard_map/reshape | solution.py:22
  154.8 23.0 %copy.12 = bf16[128,128,4,256]{3,1,2,0:T(8,128)(2,1)} copy(bf16[128,128,4,256]{3,2,1,0:T(4,128)(2,1)} %reshape.19) | data formatting | bytes 67108864 | tf_op jit(solution)/shard_map/while | solution.py:46
  177.9 0.0 copy-start.2
  177.9 0.0 copy-start.3
  177.9 4.2 %broadcast_in_dim.53 = f32[64,128,256]{2,1,0:T(8,128)} broadcast(f32[]{:T(128)} %constant.55.clone.1), dimensions={} | broadcast | bytes 8388612 | tf_op jit(solution)/shard_map/broadcast_in_dim | solution.py:32
  182.1 0.0 copy-done.2
  182.1 0.0 copy-done.3
  182.1 97.6 %while.13 = (s32[]{:T(128)}, f32[64,128,256]{2,1,0:T(8,128)}, s32[192]{0:T(256)S(1)}, pred[192]{0:T(512)(128)(4,1)S(1)}, bf16[192,128,128]{2,1,0:T(8,128)(2,1)},...) while((s32[]{:T(128)}, f32[64,128,256]{2,1,0:T(8,128)}, ...), condition=%wide.region_4.5_spmd, body=%wide.region_2.4_spmd.sunk | while | flops 541066112 | bytes 48236912 | solution.py:46
  182.1 0.1 compare_select_fusion.4
  182.2 5.2 %gather_fusion = bf16[64,128,256]{2,1,0:T(8,128)(2,1)} fusion(bf16[128,128,4,256]{3,1,2,0:T(8,128)(2,1)} %get-tuple-element.271, s32[64]{0:T(128)S(1)} %get-tuple-element.239), kind=kCustom, calls=%fused_computation.clone.1 | custom fusion | bytes 8389120 | tf_op jit(solution)/shard_map/while/body/eval_jaxpr/gather | solution.py:41
  187.3 0.1 dynamic_slice.45
  187.4 7.6 %broadcast_select_fusion.2 = f32[64,128,256]{2,1,0:T(8,128)} fusion(pred[64]{0:T(512)(128)(4,1)S(1)} %dynamic_slice.45, bf16[64,128,256]{2,1,0:T(8,128)(2,1)} %gather_fusion, bf16[192,128,128]{2,1,0:T(8,128)(2,1)} %get-tuple-element.268, s32[]{:T(128)S(6)} %select_n.61), kind=kOutput, calls=%fused_computation.2.clone.1 | convolution fusion | flops 538968064 | bytes 14680132 | tf_op jit(solution)/shard_map/while/body/eval_jaxpr/kab,kaf->kbf/dot_general | solution.py:42
  195.0 19.6 %scatter_fusion = f32[64,128,256]{2,1,0:T(8,128)} fusion(f32[64,128,256]{2,1,0:T(8,128)} %get-tuple-element.253, s32[64]{0:T(128)S(1)} %get-tuple-element.238, f32[64,128,256]{2,1,0:T(8,128)} %broadcast_select_fusion.2), kind=kCustom, calls=%fused_computation.1.clone.1 | custom fusion | flops 2097152 | bytes 25166080 | tf_op jit(solution)/shard_map/while/body/eval_jaxpr/scatter-add | solution.py:44
  214.6 0.1 compare_select_fusion.4
  214.7 5.4 %gather_fusion = bf16[64,128,256]{2,1,0:T(8,128)(2,1)} fusion(bf16[128,128,4,256]{3,1,2,0:T(8,128)(2,1)} %get-tuple-element.271, s32[64]{0:T(128)S(1)} %get-tuple-element.239), kind=kCustom, calls=%fused_computation.clone.1 | custom fusion | bytes 8389120 | tf_op jit(solution)/shard_map/while/body/eval_jaxpr/gather | solution.py:41
  220.1 0.1 dynamic_slice.45
  220.2 7.6 %broadcast_select_fusion.2 = f32[64,128,256]{2,1,0:T(8,128)} fusion(pred[64]{0:T(512)(128)(4,1)S(1)} %dynamic_slice.45, bf16[64,128,256]{2,1,0:T(8,128)(2,1)} %gather_fusion, bf16[192,128,128]{2,1,0:T(8,128)(2,1)} %get-tuple-element.268, s32[]{:T(128)S(6)} %select_n.61), kind=kOutput, calls=%fused_computation.2.clone.1 | convolution fusion | flops 538968064 | bytes 14680132 | tf_op jit(solution)/shard_map/while/body/eval_jaxpr/kab,kaf->kbf/dot_general | solution.py:42
  227.8 19.6 %scatter_fusion = f32[64,128,256]{2,1,0:T(8,128)} fusion(f32[64,128,256]{2,1,0:T(8,128)} %get-tuple-element.253, s32[64]{0:T(128)S(1)} %get-tuple-element.238, f32[64,128,256]{2,1,0:T(8,128)} %broadcast_select_fusion.2), kind=kCustom, calls=%fused_computation.1.clone.1 | custom fusion | flops 2097152 | bytes 25166080 | tf_op jit(solution)/shard_map/while/body/eval_jaxpr/scatter-add | solution.py:44
  247.3 0.1 compare_select_fusion.4
  247.4 5.3 %gather_fusion = bf16[64,128,256]{2,1,0:T(8,128)(2,1)} fusion(bf16[128,128,4,256]{3,1,2,0:T(8,128)(2,1)} %get-tuple-element.271, s32[64]{0:T(128)S(1)} %get-tuple-element.239), kind=kCustom, calls=%fused_computation.clone.1 | custom fusion | bytes 8389120 | tf_op jit(solution)/shard_map/while/body/eval_jaxpr/gather | solution.py:41
  252.7 0.1 dynamic_slice.45
  252.8 7.6 %broadcast_select_fusion.2 = f32[64,128,256]{2,1,0:T(8,128)} fusion(pred[64]{0:T(512)(128)(4,1)S(1)} %dynamic_slice.45, bf16[64,128,256]{2,1,0:T(8,128)(2,1)} %gather_fusion, bf16[192,128,128]{2,1,0:T(8,128)(2,1)} %get-tuple-element.268, s32[]{:T(128)S(6)} %select_n.61), kind=kOutput, calls=%fused_computation.2.clone.1 | convolution fusion | flops 538968064 | bytes 14680132 | tf_op jit(solution)/shard_map/while/body/eval_jaxpr/kab,kaf->kbf/dot_general | solution.py:42
  260.3 19.4 %scatter_fusion = f32[64,128,256]{2,1,0:T(8,128)} fusion(f32[64,128,256]{2,1,0:T(8,128)} %get-tuple-element.253, s32[64]{0:T(128)S(1)} %get-tuple-element.238, f32[64,128,256]{2,1,0:T(8,128)} %broadcast_select_fusion.2), kind=kCustom, calls=%fused_computation.1.clone.1 | custom fusion | flops 2097152 | bytes 25166080 | tf_op jit(solution)/shard_map/while/body/eval_jaxpr/scatter-add | solution.py:44
  279.7 0.0 copy-start.1
  279.7 6.0 %convert_element_type.17 = bf16[64,128,256]{2,1,0:T(8,128)(2,1)} convert(f32[64,128,256]{2,1,0:T(8,128)} %get-tuple-element.144) | non-fusion elementwise | flops 2097152 | bytes 12582912 | tf_op jit(solution)/shard_map/convert_element_type | solution.py:48
  285.7 0.0 reduce-scatter.2.cloned.1.call-update
  285.8 38.0 %reduce-scatter.2.cloned.1.call-done = bf16[1024,256]{1,0:T(8,128)(2,1)} async-done(((bf16[8192,256]{1,0:T(8,128)(2,1)}), bf16[1024,256]{1,0:T(8,128)(2,1)}) %reduce-scatter.2.cloned.1.call-update) | async-done | bytes 524304 | tf_op jit(solution)/shard_map/reduce_scatter | solution.py:47
  323.8 2.1 convert_element_type.19
  325.9 0.0 copy-done.1
  (1 shorter events, 0.0 us)
Async XLA Ops:
  6.5 76.1 %copy-start = (bf16[4,256,256]{2,1,0:T(8,128)(2,1)S(1)}, bf16[4,256,256]{2,1,0:T(8,128)(2,1)}, u32[]{:S(2)}) copy-start(bf16[4,256,256]{2,1,0:T(8,128)(2,1)} %param.9) | copy-start | bytes 1572868
  6.5 76.1 %all-gather.2.cloned.1.call-start = ((), (), s32[]{:S(2)}) async-start(), calls=%async_computation.1 | async-start | bytes 8912896 | tf_op jit(solution)/shard_map/all_gather | solution.py:18
  7.3 316.5 %reduce-scatter.2.cloned.1.call-start = ((), (), s32[]{:S(2)}) async-start(), calls=%async_computation.2 | async-start | bytes 4718592 | tf_op jit(solution)/shard_map/reduce_scatter | solution.py:47
  177.9 4.2 %copy-start.2 = (s32[192]{0:T(256)S(1)}, s32[192]{0:T(256)}, u32[]{:S(2)}) copy-start(s32[192]{0:T(256)} %param.12) | copy-start | bytes 2308
  177.9 4.2 %copy-start.3 = (s32[192]{0:T(256)S(1)}, s32[192]{0:T(256)}, u32[]{:S(2)}) copy-start(s32[192]{0:T(256)} %param.11) | copy-start | bytes 2308
  279.7 46.1 %copy-start.1 = (bf16[4,256,256]{2,1,0:T(8,128)(2,1)S(1)}, bf16[4,256,256]{2,1,0:T(8,128)(2,1)}, u32[]{:S(2)}) copy-start(bf16[4,256,256]{2,1,0:T(8,128)(2,1)} %param.9) | copy-start | bytes 1572868
Sparse Core Ops, SparseCore 0:
  9.5 73.1 all-gather.1
  285.9 37.8 reduce-scatter.1
where the time goes:
time: 335 us; the launch traced here: 333 us
  waiting for transfers between devices  112 us (33%)
  local copies, waits for them, and re-layouts  98.6 us (29%)
  other arithmetic  68.4 us (20%)
  matrix products  40.1 us (12%)
  between operations  13.4 us (4%)
    all_gather x1, waiting for transfers between devices, per_device(): lax.all_gather(grad_out, 'col', axis=0, tiled=True)  73.3 us
    scatter-add x3, other arithmetic, step(): return partial_value.at[col_part].add(term)  58.6 us
    reshape x1, local copies, waits for them, and re-layouts, per_device(): table = gathered.reshape(ncols * owned, blk, kinds, feat)  54.7 us
    reduce_scatter x1, waiting for transfers between devices, per_device(): lax.psum_scatter(partial_value.reshape(nrows * owned * blk, feat).astype(...  38 us
    while x1, local copies, waits for them, and re-layouts, per_device(): partial_value = lax.fori_loop(0, groups, step, partial_start)  23 us
    dot_general x3, matrix products, step(): jnp.einsum('kab,kaf->kbf', adj_part, picked, preferred_element_type=jnp.f...  22.7 us
    dot_general x1, matrix products, per_device(): jnp.dot(lax.all_gather(grad_out, 'col', axis=0, tiled=True), wcat, prefer...  17.5 us
    gather x3, local copies, waits for them, and re-layouts, step(): picked = table[slot_part, :, kind_part, :]  15.9 us
  transfers between devices with their start and end apart: 2, of which 2 were waited for; matrix products, arithmetic and copies ran while one was open for 1% of the time, Pallas kernels for 0%

commit v1 on v0

--- a/solution.py
+++ b/solution.py
@@ -15,7 +15,10 @@
     slots_total = adjacency.shape[0]
     wcat = jnp.transpose(rel_weight, (2, 0, 1)).reshape(feat, kinds * feat)
     gathered = jnp.dot(
-        lax.all_gather(grad_out, "col", axis=0, tiled=True),
+        jnp.concatenate(
+            lax.all_to_all(jnp.stack([grad_out] * lax.axis_size("col"), axis=0), "col", 0, 0),
+            axis=0,
+        ),
         wcat,
         preferred_element_type=jnp.float32,
     ).astype(jnp.bfloat16)

time: 335 us -> 396 us (1.18)
  waiting for transfers between devices: 112 us -> 162 us
  starting transfers between devices: 0.04 us -> 7.37 us
  local copies, waits for them, and re-layouts: 98.6 us -> 104 us
    all_to_all x0 -> x1, waiting for transfers between devices: none -> 123 us  [per_device(): lax.all_to_all(jnp.stack([grad_out] * lax.axis_size('col'), axis=0), 'col...]
    all_gather x1 -> x0, waiting for transfers between devices: 73.3 us -> none  [per_device(): lax.all_gather(grad_out, 'col', axis=0, tiled=True)]
    all_to_all x0 -> x1, starting transfers between devices: none -> 7.33 us  [per_device(): lax.all_to_all(jnp.stack([grad_out] * lax.axis_size('col'), axis=0), 'col...]
    another operation x0 -> x1, local copies, waits for them, and re-layouts: none -> 5.12 us  [per_device(): jnp.stack([grad_out] * lax.axis_size('col'), axis=0)]
  transfers between devices with their start and end apart: 2 -> 2, of which waited for: 2 -> 2; matrix products, arithmetic and copies ran while one was open for 1% -> 0% of each run, Pallas kernels for 0% -> 0%
where the time goes in v1:
time: 396 us; the launch traced here: 394 us
  waiting for transfers between devices  162 us (41%)
  local copies, waits for them, and re-layouts  104 us (26%)
  other arithmetic  67.9 us (17%)
  matrix products  40.1 us (10%)
  between operations  13.4 us (3%)
  starting transfers between devices  7.37 us (2%)
    all_to_all x1, waiting for transfers between devices, per_device(): lax.all_to_all(jnp.stack([grad_out] * lax.axis_size('col'), axis=0), 'col...  123 us
    scatter-add x3, other arithmetic, step(): return partial_value.at[col_part].add(term)  58.6 us
    reshape x1, local copies, waits for them, and re-layouts, per_device(): table = gathered.reshape(ncols * owned, blk, kinds, feat)  54.7 us
    reduce_scatter x1, waiting for transfers between devices, per_device(): lax.psum_scatter(partial_value.reshape(nrows * owned * blk, feat).astype(...  38.9 us
    while x1, local copies, waits for them, and re-layouts, per_device(): partial_value = lax.fori_loop(0, groups, step, partial_start)  23 us
    dot_general x3, matrix products, step(): jnp.einsum('kab,kaf->kbf', adj_part, picked, preferred_element_type=jnp.f...  22.7 us
    dot_general x1, matrix products, per_device(): jnp.dot(jnp.concatenate(lax.all_to_all(jnp.stack([grad_out] * lax.axis_si...  17.5 us
    gather x3, local copies, waits for them, and re-layouts, step(): picked = table[slot_part, :, kind_part, :]  15.9 us
  transfers between devices with their start and end apart: 2, of which 2 were waited for; matrix products, arithmetic and copies ran while one was open for 0% of the time, Pallas kernels for 0%

profile of v1, /device:TPU:0, one launch (start us, length us, event | category | flops | bytes accessed | tf_op | source)
XLA Modules:
  0.0 394.1 jit_solution(15003053328651732664)
XLA Ops:
  6.5 0.0 copy-start
  6.5 5.1 %stack.2 = bf16[16,1024,256]{2,1,0:T(8,128)(2,1)} broadcast(bf16[1024,256]{1,0:T(8,128)(2,1)} %param.8), dimensions={1,2} | broadcast | bytes 8912896 | tf_op jit(solution)/shard_map/stack | solution.py:19
  11.7 0.0 copy-start.4
  11.7 7.3 %all-to-all-start = ((bf16[16,1024,256]{2,1,0:T(8,128)(2,1)}), bf16[16,1024,256]{2,1,0:T(8,128)(2,1)}, u32[]{:S(2)}, u32[]{:S(2)}) async-start(bf16[16,1024,256]{2,1,0:T(8,128)(2,1)} %stack.2), calls=%async_computation | async-start | bytes 16777216 | tf_op jit(solution)/shard_map/all_to_all | solution.py:19
  19.0 0.0 reduce-scatter.2.cloned.1.call-start
  19.0 0.0 copy-done.4
  19.1 0.2 reduce-window.4
  19.2 0.6 slice.4
  19.8 0.6 iota_compare_fusion.1
  20.5 0.1 convert_reduce_fusion
  20.6 122.6 %all-to-all-done = bf16[16,1024,256]{2,1,0:T(8,128)(2,1)} async-done(((bf16[16,1024,256]{2,1,0:T(8,128)(2,1)}), bf16[16,1024,256]{2,1,0:T(8,128)(2,1)}, u32[]{:S(2)}, u32[]{:S(2)}) %all-to-all-start) | async-done | bytes 8388640 | tf_op jit(solution)/shard_map/all_to_all | solution.py:19
  143.2 0.0 copy-done
  143.2 17.5 %convolution_convert_fusion = bf16[16384,1024]{1,0:T(8,128)(2,1)} fusion(bf16[16384,256]{1,0:T(8,128)(2,1)} %bitcast.3, bf16[256,1024]{0,1:T(8,128)(2,1)S(1)} %bitcast.13), kind=kOutput, calls=%fused_computation.13 | convolution fusion | flops 8606711808 | bytes 42467328 | tf_op jit(solution)/shard_map/dot_general | solution.py:17
  160.6 54.7 %reshape.25 = bf16[128,128,4,256]{3,2,1,0:T(4,128)(2,1)} reshape(bf16[16384,1024]{1,0:T(8,128)(2,1)} %convolution_convert_fusion) | data formatting | bytes 67108864 | tf_op jit(solution)/shard_map/reshape | solution.py:25
  215.3 23.0 %copy.12 = bf16[128,128,4,256]{3,1,2,0:T(8,128)(2,1)} copy(bf16[128,128,4,256]{3,2,1,0:T(4,128)(2,1)} %reshape.25) | data formatting | bytes 67108864 | tf_op jit(solution)/shard_map/while | solution.py:49
  238.3 0.0 copy-start.2
  238.3 0.0 copy-start.3
  238.3 4.2 %broadcast_in_dim.53 = f32[64,128,256]{2,1,0:T(8,128)} broadcast(f32[]{:T(128)} %constant.55.clone.1), dimensions={} | broadcast | bytes 8388612 | tf_op jit(solution)/shard_map/broadcast_in_dim | solution.py:35
  242.6 0.0 copy-done.2
  242.6 0.0 copy-done.3
  242.6 97.6 %while.13 = (s32[]{:T(128)}, f32[64,128,256]{2,1,0:T(8,128)}, s32[192]{0:T(256)S(1)}, pred[192]{0:T(512)(128)(4,1)S(1)}, bf16[192,128,128]{2,1,0:T(8,128)(2,1)},...) while((s32[]{:T(128)}, f32[64,128,256]{2,1,0:T(8,128)}, ...), condition=%wide.region_4.5_spmd, body=%wide.region_2.4_spmd.sunk | while | flops 541066112 | bytes 48236912 | solution.py:49
  242.6 0.1 compare_select_fusion.4
  242.7 5.2 %gather_fusion = bf16[64,128,256]{2,1,0:T(8,128)(2,1)} fusion(bf16[128,128,4,256]{3,1,2,0:T(8,128)(2,1)} %get-tuple-element.271, s32[64]{0:T(128)S(1)} %get-tuple-element.239), kind=kCustom, calls=%fused_computation.clone.1 | custom fusion | bytes 8389120 | tf_op jit(solution)/shard_map/while/body/eval_jaxpr/gather | solution.py:44
  247.8 0.1 dynamic_slice.45
  247.9 7.6 %broadcast_select_fusion.2 = f32[64,128,256]{2,1,0:T(8,128)} fusion(pred[64]{0:T(512)(128)(4,1)S(1)} %dynamic_slice.45, bf16[64,128,256]{2,1,0:T(8,128)(2,1)} %gather_fusion, bf16[192,128,128]{2,1,0:T(8,128)(2,1)} %get-tuple-element.268, s32[]{:T(128)S(6)} %select_n.61), kind=kOutput, calls=%fused_computation.2.clone.1 | convolution fusion | flops 538968064 | bytes 14680132 | tf_op jit(solution)/shard_map/while/body/eval_jaxpr/kab,kaf->kbf/dot_general | solution.py:45
  255.5 19.6 %scatter_fusion = f32[64,128,256]{2,1,0:T(8,128)} fusion(f32[64,128,256]{2,1,0:T(8,128)} %get-tuple-element.253, s32[64]{0:T(128)S(1)} %get-tuple-element.238, f32[64,128,256]{2,1,0:T(8,128)} %broadcast_select_fusion.2), kind=kCustom, calls=%fused_computation.1.clone.1 | custom fusion | flops 2097152 | bytes 25166080 | tf_op jit(solution)/shard_map/while/body/eval_jaxpr/scatter-add | solution.py:47
  275.1 0.1 compare_select_fusion.4
  275.2 5.4 %gather_fusion = bf16[64,128,256]{2,1,0:T(8,128)(2,1)} fusion(bf16[128,128,4,256]{3,1,2,0:T(8,128)(2,1)} %get-tuple-element.271, s32[64]{0:T(128)S(1)} %get-tuple-element.239), kind=kCustom, calls=%fused_computation.clone.1 | custom fusion | bytes 8389120 | tf_op jit(solution)/shard_map/while/body/eval_jaxpr/gather | solution.py:44
  280.6 0.1 dynamic_slice.45
  280.7 7.6 %broadcast_select_fusion.2 = f32[64,128,256]{2,1,0:T(8,128)} fusion(pred[64]{0:T(512)(128)(4,1)S(1)} %dynamic_slice.45, bf16[64,128,256]{2,1,0:T(8,128)(2,1)} %gather_fusion, bf16[192,128,128]{2,1,0:T(8,128)(2,1)} %get-tuple-element.268, s32[]{:T(128)S(6)} %select_n.61), kind=kOutput, calls=%fused_computation.2.clone.1 | convolution fusion | flops 538968064 | bytes 14680132 | tf_op jit(solution)/shard_map/while/body/eval_jaxpr/kab,kaf->kbf/dot_general | solution.py:45
  288.2 19.6 %scatter_fusion = f32[64,128,256]{2,1,0:T(8,128)} fusion(f32[64,128,256]{2,1,0:T(8,128)} %get-tuple-element.253, s32[64]{0:T(128)S(1)} %get-tuple-element.238, f32[64,128,256]{2,1,0:T(8,128)} %broadcast_select_fusion.2), kind=kCustom, calls=%fused_computation.1.clone.1 | custom fusion | flops 2097152 | bytes 25166080 | tf_op jit(solution)/shard_map/while/body/eval_jaxpr/scatter-add | solution.py:47
  307.8 0.1 compare_select_fusion.4
  307.9 5.3 %gather_fusion = bf16[64,128,256]{2,1,0:T(8,128)(2,1)} fusion(bf16[128,128,4,256]{3,1,2,0:T(8,128)(2,1)} %get-tuple-element.271, s32[64]{0:T(128)S(1)} %get-tuple-element.239), kind=kCustom, calls=%fused_computation.clone.1 | custom fusion | bytes 8389120 | tf_op jit(solution)/shard_map/while/body/eval_jaxpr/gather | solution.py:44
  313.2 0.1 dynamic_slice.45
  313.2 7.6 %broadcast_select_fusion.2 = f32[64,128,256]{2,1,0:T(8,128)} fusion(pred[64]{0:T(512)(128)(4,1)S(1)} %dynamic_slice.45, bf16[64,128,256]{2,1,0:T(8,128)(2,1)} %gather_fusion, bf16[192,128,128]{2,1,0:T(8,128)(2,1)} %get-tuple-element.268, s32[]{:T(128)S(6)} %select_n.61), kind=kOutput, calls=%fused_computation.2.clone.1 | convolution fusion | flops 538968064 | bytes 14680132 | tf_op jit(solution)/shard_map/while/body/eval_jaxpr/kab,kaf->kbf/dot_general | solution.py:45
  320.8 19.4 %scatter_fusion = f32[64,128,256]{2,1,0:T(8,128)} fusion(f32[64,128,256]{2,1,0:T(8,128)} %get-tuple-element.253, s32[64]{0:T(128)S(1)} %get-tuple-element.238, f32[64,128,256]{2,1,0:T(8,128)} %broadcast_select_fusion.2), kind=kCustom, calls=%fused_computation.1.clone.1 | custom fusion | flops 2097152 | bytes 25166080 | tf_op jit(solution)/shard_map/while/body/eval_jaxpr/scatter-add | solution.py:47
  340.2 0.0 copy-start.1
  340.2 6.0 %convert_element_type.17 = bf16[64,128,256]{2,1,0:T(8,128)(2,1)} convert(f32[64,128,256]{2,1,0:T(8,128)} %get-tuple-element.144) | non-fusion elementwise | flops 2097152 | bytes 12582912 | tf_op jit(solution)/shard_map/convert_element_type | solution.py:51
  346.2 0.0 reduce-scatter.2.cloned.1.call-update
  346.2 38.9 %reduce-scatter.2.cloned.1.call-done = bf16[1024,256]{1,0:T(8,128)(2,1)} async-done(((bf16[8192,256]{1,0:T(8,128)(2,1)}), bf16[1024,256]{1,0:T(8,128)(2,1)}) %reduce-scatter.2.cloned.1.call-update) | async-done | bytes 524304 | tf_op jit(solution)/shard_map/reduce_scatter | solution.py:50
  385.2 2.1 convert_element_type.19
  387.2 0.0 copy-done.1
  (1 shorter events, 0.0 us)
Async XLA Ops:
  6.5 136.6 %copy-start = (bf16[4,256,256]{2,1,0:T(8,128)(2,1)S(1)}, bf16[4,256,256]{2,1,0:T(8,128)(2,1)}, u32[]{:S(2)}) copy-start(bf16[4,256,256]{2,1,0:T(8,128)(2,1)} %param.9) | copy-start | bytes 1572868
  11.7 7.4 %copy-start.4 = (s32[4]{0:T(128)S(1)}, s32[4]{0:T(128)}, u32[]{:S(2)}) copy-start(s32[4]{0:T(128)} %param.13) | copy-start | bytes 52
  11.7 131.5 %all-to-all-start = ((bf16[16,1024,256]{2,1,0:T(8,128)(2,1)}), bf16[16,1024,256]{2,1,0:T(8,128)(2,1)}, u32[]{:S(2)}, u32[]{:S(2)}) async-start(bf16[16,1024,256]{2,1,0:T(8,128)(2,1)} %stack.2), calls=%async_computation | async-start | bytes 16777216 | tf_op jit(solution)/shard_map/all_to_all | solution.py:19
  19.0 366.2 %reduce-scatter.2.cloned.1.call-start = ((), (), s32[]{:S(2)}) async-start(), calls=%async_computation.2 | async-start | bytes 4718592 | tf_op jit(solution)/shard_map/reduce_scatter | solution.py:50
  238.3 4.2 %copy-start.2 = (s32[192]{0:T(256)S(1)}, s32[192]{0:T(256)}, u32[]{:S(2)}) copy-start(s32[192]{0:T(256)} %param.12) | copy-start | bytes 2308
  238.3 4.2 %copy-start.3 = (s32[192]{0:T(256)S(1)}, s32[192]{0:T(256)}, u32[]{:S(2)}) copy-start(s32[192]{0:T(256)} %param.11) | copy-start | bytes 2308
  340.2 47.0 %copy-start.1 = (bf16[4,256,256]{2,1,0:T(8,128)(2,1)S(1)}, bf16[4,256,256]{2,1,0:T(8,128)(2,1)}, u32[]{:S(2)}) copy-start(bf16[4,256,256]{2,1,0:T(8,128)(2,1)} %param.9) | copy-start | bytes 1572868
Sparse Core Ops, SparseCore 0:
  346.4 38.7 reduce-scatter.1
